TPU v7x, 32 devices: a whole 2x2x4 slice. The times are simulated.
32 devices in a mesh: section: 2 (over core), seq: 4 (over y, x), mp: 4 (over z).
Axes of the slice: x: 2, y: 2, z: 4, core: 2. Of those that a mesh axis runs over, the one named last changes fastest.
Arguments:
- token_ids: int32 [2, 1024], P(None, 'seq'), may hold values from 0 to 511
- embed_table: bfloat16 [512, 4096], P(None, 'mp'), may hold values from -40 to 40
- norm_gain: bfloat16 [2, 4096], P('section', 'mp'), may hold values from 0.099609375 to 1.8984375
- short_filters: bfloat16 [2, 3, 7, 4096], P('section', None, None, 'mp'), may hold values from -2 to 2
- medium_filters: bfloat16 [2, 128, 4096], P('section', None, 'mp'), may hold values from -0.5 to 0.5
- out_weight: bfloat16 [2, 4096, 4096], P('section', 'seq', 'mp'), may hold values from -0.09375 to 0.09375
Outputs:
- streams: bfloat16 [2, 2, 1024, 4096], P('section', None, 'seq', 'mp')
All inputs are finite; a program needn't handle non-finite values.
Results may differ from a plain program's by a relative error of at most 0.018.
Values may be sent and summed in bfloat16 or wider, within the bound.
A program may use at most 64 MiB of HBM per device.

v0:
```python
import jax
import jax.numpy as jnp
from jax import lax
from jax.sharding import PartitionSpec as P

D = 4096


def passed_along(value, axis, by):
    devices = lax.axis_size(axis)
    pairs = [(i, i + by) for i in range(devices) if 0 <= i + by < devices]
    return lax.ppermute(value, axis, pairs)


def depthwise(extended, taps):
    kernel = jnp.flip(taps, 0)[:, None, :]
    result = lax.conv_general_dilated(
        extended[None],
        kernel,
        (1,),
        "VALID",
        dimension_numbers=("NWC", "WIO", "NWC"),
        feature_group_count=taps.shape[1],
        preferred_element_type=jnp.float32,
    )
    return result[0]


def mixer_layer(stream_in, gain, shorts, medium, weight_cols):
    rows = stream_in.shape[0]
    stream = stream_in.astype(jnp.float32)
    own_squares = jnp.sum(stream * stream, axis=1, keepdims=True)
    all_squares = lax.psum(own_squares, "mp")
    normed = (
        stream * lax.rsqrt(all_squares / D + 1e-06) * gain.astype(jnp.float32)[None, :]
    ).astype(jnp.bfloat16)
    short_span = shorts.shape[1] - 1
    medium_span = medium.shape[0] - 1
    lower_rim = passed_along(normed[rows - short_span :], "seq", 1)
    extended = jnp.concatenate([lower_rim, normed], axis=0)
    features = [depthwise(extended, shorts[index]).astype(jnp.bfloat16) for index in range(3)]
    product = (features[1].astype(jnp.float32) * features[2].astype(jnp.float32)).astype(
        jnp.bfloat16
    )
    product_rim = passed_along(product[rows - medium_span :], "seq", 1)
    filtered = depthwise(jnp.concatenate([product_rim, product], axis=0), medium)
    query = features[0]
    gated = (query.astype(jnp.float32) * filtered).astype(jnp.bfloat16)
    empty = jnp.zeros((rows, weight_cols.shape[1]), jnp.float32)
    piece = jax.tree.map(lambda a: lax.all_gather(a, "mp", axis=1, tiled=True), gated)
    block_rows = lax.slice_in_dim(weight_cols, 0, piece.shape[1], axis=0)
    projected = empty + jnp.dot(piece, block_rows, preferred_element_type=jnp.float32)
    return (stream + projected).astype(jnp.bfloat16)


def local(token_ids, embed_table, norm_gain, short_filters, medium_filters, out_weight):
    section_index = lax.axis_index("section")
    weight_cols = lax.all_gather(out_weight, "seq", axis=1, tiled=True)[0]
    gain = norm_gain[0]
    shorts = short_filters[0]
    medium = medium_filters[0]
    micro_count = token_ids.shape[0]
    rows = token_ids.shape[1]
    width = embed_table.shape[1]
    vocab_ids = lax.broadcasted_iota(jnp.int32, (rows, embed_table.shape[0]), 1)
    received = jnp.zeros((rows, width), jnp.bfloat16)
    results = []
    for tick_index in range(micro_count + 1):
        chosen = token_ids[min(tick_index, micro_count - 1)]
        one_hot = (chosen[:, None] == vocab_ids).astype(jnp.bfloat16)
        embedded = jnp.dot(one_hot, embed_table, preferred_element_type=jnp.float32).astype(
            jnp.bfloat16
        )
        stream_in = jnp.where(section_index == 0, embedded, received)
        result = mixer_layer(stream_in, gain, shorts, medium, weight_cols)
        results.append(result)
        if tick_index < micro_count:
            received = passed_along(result, "section", 1)
    ordered = [
        jnp.where(section_index == 0, results[index], results[index + 1])
        for index in range(micro_count)
    ]
    return jnp.stack(ordered)[None]


def solution(mesh):
    in_specs = (
        P(None, "seq"),
        P(None, "mp"),
        P("section", "mp"),
        P("section", None, None, "mp"),
        P("section", None, "mp"),
        P("section", "seq", "mp"),
    )
    out_specs = P("section", None, "seq", "mp")
    return jax.shard_map(local, mesh=mesh, in_specs=in_specs, out_specs=out_specs, check_vma=False)
```

profile of v0, /device:TPU:0, one launch (start us, length us, event | category | flops | bytes accessed | tf_op | source)
XLA Modules:
  0.0 514.0 jit_solution(5375181700684785683)
XLA Ops:
  8.6 13.5 %psum.21 = f32[256,1]{0,1:T(1,128)S(1)} all-reduce(f32[256,1]{0,1:T(1,128)S(1)} %bitcast.136), channel_id=1, replica_groups=mesh['section'=2,'seq'=4,'mp'=4] {'mp'}, use_global_device_ids=true, to_apply=%region_1.2 | all-reduce | flops 256 | bytes 2048 | tf_op jit(solution)/shard_map/psum | solution.py:33
  22.3 3.4 collective-permute-start
  26.5 2.6 rev.25
  32.5 4.1 collective-permute-start.1
  37.9 2.3 reshape.126
  40.2 1.2 maximum_bitcast_fusion.1
  41.5 15.2 %fusion.86 = bf16[1,256,1024]{2,0,1:T(2,128)(2,1)} fusion(bf16[1,383,1024]{2,1,0:T(8,128)(2,1)S(1)} %maximum_bitcast_fusion.1, f32[1,264,1024]{2,0,1:T(1,128)S(1)} %copy-done.2, bf16[128,1,1024]{2,0,1:T(8,128)(2,1)S(1)} %bitcast.116), kind=kOutput, calls=%fused_computation.73 | convolution fusion | flops 67633152 | bytes 2619392 | tf_op jit(solution)/shard_map/conv_general_dilated | solution.py:17
  58.0 78.3 %all-gather.10.cloned.1.call-done = bf16[1,256,4096]{2,0,1:T(2,128)(2,1)} async-done(((bf16[1,256,1024]{2,0,1:T(2,128)(2,1)}), bf16[1,256,4096]{2,0,1:T(2,128)(2,1)}) %all-gather.10.cloned.1.call-update) | async-done | bytes 2097168 | tf_op jit(solution)/shard_map/all_gather | solution.py:50
  136.3 87.5 %all-gather.8.cloned.1.call-done = bf16[1,4096,1024]{2,1,0:T(8,128)(2,1)} async-done(((bf16[1,1024,1024]{2,1,0:T(8,128)(2,1)}), bf16[1,4096,1024]{2,1,0:T(8,128)(2,1)}) %all-gather.8.cloned.1.call-update) | async-done | bytes 8388624 | tf_op jit(solution)/shard_map/all_gather | solution.py:58
  223.8 8.6 %fusion.54 = bf16[256,1024]{1,0:T(8,128)(2,1)S(1)} fusion(bf16[1,4096,1024]{2,1,0:T(8,128)(2,1)} %all-gather.8.cloned.1.call-done, bf16[1,256,4096]{2,0,1:T(2,128)(2,1)} %all-gather.10.cloned.1.call-done, bf16[256,1024]{1,0:T(8,128)(2,1)S(1)} %get-tuple-element.15), kind=kOutput, calls=%fused_computation.62 | convolution fusion | flops 2148270080 | bytes 11534336 | tf_op jit(solution)/shard_map/dot_general | solution.py:52
  232.5 1.6 collective-permute-start.2
  234.1 1.5 collective-permute-done.2
  236.2 11.7 %psum.22 = f32[256,1]{0,1:T(1,128)S(1)} all-reduce(f32[256,1]{0,1:T(1,128)S(1)} %bitcast.135), channel_id=1, replica_groups=mesh['section'=2,'seq'=4,'mp'=4] {'mp'}, use_global_device_ids=true, to_apply=%region_3.4 | all-reduce | flops 256 | bytes 2048 | tf_op jit(solution)/shard_map/psum | solution.py:33
  248.1 3.4 collective-permute-start.3
  251.5 1.4 collective-permute-done.3
  256.2 4.9 collective-permute-start.4
  262.3 1.3 reshape.127
  264.6 1.1 maximum_bitcast_fusion.2
  265.7 15.2 %fusion.92 = bf16[1,256,1024]{2,0,1:T(2,128)(2,1)} fusion(bf16[1,383,1024]{2,1,0:T(8,128)(2,1)S(1)} %maximum_bitcast_fusion.2, f32[1,264,1024]{2,0,1:T(1,128)S(1)} %reshape.127, bf16[128,1,1024]{2,0,1:T(8,128)(2,1)S(1)} %bitcast.117), kind=kOutput, calls=%fused_computation.75 | convolution fusion | flops 67633152 | bytes 2619392 | tf_op jit(solution)/shard_map/conv_general_dilated | solution.py:17
  281.1 80.5 %all-gather.12.cloned.1.call-done = bf16[1,256,4096]{2,0,1:T(2,128)(2,1)} async-done(((bf16[1,256,1024]{2,0,1:T(2,128)(2,1)}), bf16[1,256,4096]{2,0,1:T(2,128)(2,1)}) %all-gather.12.cloned.1.call-update) | async-done | bytes 2097168 | tf_op jit(solution)/shard_map/all_gather | solution.py:50
  361.6 8.6 %fusion.59 = bf16[256,1024]{1,0:T(8,128)(2,1)S(1)} fusion(bf16[1,4096,1024]{2,1,0:T(8,128)(2,1)} %all-gather.8.cloned.1.call-done, bf16[1,256,4096]{2,0,1:T(2,128)(2,1)} %all-gather.12.cloned.1.call-done, bf16[256,1024]{1,0:T(8,128)(2,1)S(1)} %copy-done.4), kind=kOutput, calls=%fused_computation.63 | convolution fusion | flops 2148270080 | bytes 11534336 | tf_op jit(solution)/shard_map/dot_general | solution.py:52
  370.2 1.3 collective-permute-start.5
  371.6 1.5 collective-permute-done.5
  373.3 9.4 %psum.23 = f32[256,1]{0,1:T(1,128)S(1)} all-reduce(f32[256,1]{0,1:T(1,128)S(1)} %bitcast.131), channel_id=1, replica_groups=mesh['section'=2,'seq'=4,'mp'=4] {'mp'}, use_global_device_ids=true, to_apply=%region_5.6 | all-reduce | flops 256 | bytes 2048 | tf_op jit(solution)/shard_map/psum | solution.py:33
  382.9 3.4 collective-permute-start.6
  386.3 1.4 collective-permute-done.6
  391.0 5.1 collective-permute-start.7
  397.4 1.3 reshape.128
  399.4 1.1 maximum_bitcast_fusion.3
  400.5 15.2 %fusion.98 = bf16[1,256,1024]{2,0,1:T(2,128)(2,1)} fusion(bf16[1,383,1024]{2,1,0:T(8,128)(2,1)S(1)} %maximum_bitcast_fusion.3, f32[1,264,1024]{2,0,1:T(1,128)S(1)} %reshape.128, bf16[128,1,1024]{2,0,1:T(8,128)(2,1)S(1)} %bitcast.118), kind=kOutput, calls=%fused_computation.77 | convolution fusion | flops 67633152 | bytes 2619392 | tf_op jit(solution)/shard_map/conv_general_dilated | solution.py:17
  416.9 80.5 %all-gather.14.cloned.1.call-done = bf16[1,256,4096]{2,0,1:T(2,128)(2,1)} async-done(((bf16[1,256,1024]{2,0,1:T(2,128)(2,1)}), bf16[1,256,4096]{2,0,1:T(2,128)(2,1)}) %all-gather.14.cloned.1.call-update) | async-done | bytes 2097168 | tf_op jit(solution)/shard_map/all_gather | solution.py:50
  497.4 8.7 %fusion.78 = bf16[1,256,1024]{2,1,0:T(8,128)(2,1)S(1)} fusion(bf16[256,1024]{1,0:T(8,128)(2,1)S(1)} %copy-done.8, bf16[1,4096,1024]{2,1,0:T(8,128)(2,1)} %all-gather.8.cloned.1.call-done, bf16[1,256,4096]{2,0,1:T(2,128)(2,1)} %all-gather.14.cloned.1.call-done, bf16[256,1024]{1,0:T(8,128)(2,1)S(1)} %get-tuple-element.6, pred[]{:T(512)S(6)} %eq.14), kind=kOutput, calls=%fused_computation.71 | convolution fusion | flops 2148532224 | bytes 12058625 | tf_op jit(solution)/shard_map/dot_general | solution.py:52
  (101 shorter events, 23.4 us)
Async XLA Ops:
  6.5 1.5 copy-start
  6.5 129.7 %all-gather.10.cloned.1.call-start = ((), (), s32[]{:S(2)}) async-start(), calls=%async_computation.1 | async-start | bytes 5242880 | tf_op jit(solution)/shard_map/all_gather | solution.py:50
  8.0 17.7 %copy-start.13 = (bf16[1,3,7,1024]{3,2,1,0:T(8,128)(2,1)S(1)}, bf16[1,3,7,1024]{3,2,1,0:T(8,128)(2,1)}, u32[]{:S(2)}) copy-start(bf16[1,3,7,1024]{3,2,1,0:T(8,128)(2,1)} %param.9) | copy-start | bytes 129028
  8.0 18.5 %copy-start.9 = (bf16[1,128,1024]{2,1,0:T(8,128)(2,1)S(1)}, bf16[1,128,1024]{2,1,0:T(8,128)(2,1)}, u32[]{:S(2)}) copy-start(bf16[1,128,1024]{2,1,0:T(8,128)(2,1)} %param.10) | copy-start | bytes 786436
  22.3 6.8 %collective-permute-start = (bf16[6,1024]{1,0:T(8,128)(2,1)S(1)}, bf16[6,1024]{1,0:T(8,128)(2,1)S(1)}, u32[]{:S(2)}, u32[]{:S(2)}) collective-permute-start(bf16[6,1024]{1,0:T(8,128)(2,1)S(1)} %slice.84), channel_id=1, source_target_pairs={{0,4},{4,8},{8,12},{1,5},{5,9},{9,13},{2,6},{6,10},{10,14},{3,7},{... | collective-permute-start | bytes 36872 | tf_op jit(solution)/shard_map/ppermute | solution.py:12
  29.3 0.7 copy-start.14
  32.5 7.7 %collective-permute-start.1 = (bf16[127,1024]{1,0:T(8,128)(2,1)}, bf16[127,1024]{1,0:T(8,128)(2,1)}, u32[]{:S(2)}, u32[]{:S(2)}) collective-permute-start(bf16[127,1024]{1,0:T(8,128)(2,1)} %slice_bitcast_fusion.5), channel_id=1, source_target_pairs={{0,4},{4,8},{8,12},{1,5},{5,9},{9,13},{2,6},{6,10},{10,14},{3,7},{... | collective-permute-start | bytes 780296 | tf_op jit(solution)/shard_map/ppermute | solution.py:12
  40.2 1.3 copy-start.2
  40.2 1.4 copy-start.10
  56.7 167.1 %all-gather.8.cloned.1.call-start = ((), (), s32[]{:S(2)}) async-start(), calls=%async_computation | async-start | bytes 10485760 | tf_op jit(solution)/shard_map/all_gather | solution.py:58
  57.5 304.1 %all-gather.12.cloned.1.call-start = ((), (), s32[]{:S(2)}) async-start(), calls=%async_computation.2 | async-start | bytes 5242880 | tf_op jit(solution)/shard_map/all_gather | solution.py:50
  232.5 3.1 copy-start.5
  232.5 3.1 collective-permute-start.2
  236.2 16.7 %copy-start.3 = (bf16[256,1024]{1,0:T(8,128)(2,1)}, bf16[256,1024]{1,0:T(8,128)(2,1)S(1)}, u32[]{:S(2)}) copy-start(bf16[256,1024]{1,0:T(8,128)(2,1)S(1)} %get-tuple-element.8) | copy-start | bytes 1572868
  248.1 4.8 collective-permute-start.3
  256.2 8.4 %collective-permute-start.4 = (bf16[127,1024]{1,0:T(8,128)(2,1)}, bf16[127,1024]{1,0:T(8,128)(2,1)}, u32[]{:S(2)}, u32[]{:S(2)}) collective-permute-start(bf16[127,1024]{1,0:T(8,128)(2,1)} %slice_bitcast_fusion.4), channel_id=1, source_target_pairs={{0,4},{4,8},{8,12},{1,5},{5,9},{9,13},{2,6},{6,10},{10,14},{3,7},{... | collective-permute-start | bytes 780296 | tf_op jit(solution)/shard_map/ppermute | solution.py:12
  263.6 2.0 copy-start.11
  265.6 95.9 %copy-start.4 = (bf16[256,1024]{1,0:T(8,128)(2,1)S(1)}, bf16[256,1024]{1,0:T(8,128)(2,1)}, u32[]{:S(2)}) copy-start(bf16[256,1024]{1,0:T(8,128)(2,1)} %copy-done.3) | copy-start | bytes 1572868
  280.9 216.5 %all-gather.14.cloned.1.call-start = ((), (), s32[]{:S(2)}) async-start(), calls=%async_computation.3 | async-start | bytes 5242880 | tf_op jit(solution)/shard_map/all_gather | solution.py:50
  370.2 12.7 %copy-start.7 = (bf16[256,1024]{1,0:T(8,128)(2,1)}, bf16[256,1024]{1,0:T(8,128)(2,1)S(1)}, u32[]{:S(2)}) copy-start(bf16[256,1024]{1,0:T(8,128)(2,1)S(1)} %fusion.59) | copy-start | bytes 1572868
  370.2 2.8 collective-permute-start.5
  382.9 4.8 collective-permute-start.6
  391.0 8.4 %collective-permute-start.7 = (bf16[127,1024]{1,0:T(8,128)(2,1)}, bf16[127,1024]{1,0:T(8,128)(2,1)}, u32[]{:S(2)}, u32[]{:S(2)}) collective-permute-start(bf16[127,1024]{1,0:T(8,128)(2,1)} %slice_bitcast_fusion.3), channel_id=1, source_target_pairs={{0,4},{4,8},{8,12},{1,5},{5,9},{9,13},{2,6},{6,10},{10,14},{3,7},{... | collective-permute-start | bytes 780296 | tf_op jit(solution)/shard_map/ppermute | solution.py:12
  398.7 1.8 copy-start.12
  415.7 1.0 copy-start.6
  415.7 1.2 copy-start.8
  497.4 9.8 %copy-start.1 = (bf16[512,1024]{1,0:T(8,128)(2,1)S(1)}, bf16[512,1024]{1,0:T(8,128)(2,1)}, u32[]{:S(2)}) copy-start(bf16[512,1024]{1,0:T(8,128)(2,1)} %param.7) | copy-start | bytes 3145732
Sparse Core Ops, SparseCore 0:
  56.8 79.4 all-gather.9
  138.1 85.6 all-gather.7
  281.0 80.5 all-gather.11
  415.8 81.5 all-gather.13
where the time goes:
time: 521 us; the launch traced here: 514 us
  waiting for transfers between devices  335 us (64%)
  matrix products  78.3 us (15%)
  blocking collectives  34.5 us (7%)
  starting transfers between devices  27.9 us (5%)
  local copies, waits for them, and re-layouts  18 us (3%)
  between operations  13.9 us (3%)
  other arithmetic  6.4 us (1%)
    all_gather x3, waiting for transfers between devices, mixer_layer(): lax.all_gather(a, 'mp', axis=1, tiled=True)  239 us
    all_gather x1, waiting for transfers between devices, local(): weight_cols = lax.all_gather(out_weight, 'seq', axis=1, tiled=True)[0]  87.5 us
    conv_general_dilated x12, matrix products, depthwise(): lax.conv_general_dilated(extended[None], kernel, (1,), 'VALID', dimension...  51.1 us
    psum x3, blocking collectives, mixer_layer(): all_squares = lax.psum(own_squares, 'mp')  34.5 us
    ppermute x8, starting transfers between devices, passed_along(): return lax.ppermute(value, axis, pairs)  27.2 us
    dot_general x3, matrix products, mixer_layer(): jnp.dot(piece, block_rows, preferred_element_type=jnp.float32)  26 us
  transfers between devices with their start and end apart: 12, of which 10 were waited for; matrix products, arithmetic and copies ran while one was open for 2% of the time, Pallas kernels for 0%

commit v1 on v0

--- a/solution.py
+++ b/solution.py
@@ -1,9 +1,39 @@
+import functools
 import jax
 import jax.numpy as jnp
 from jax import lax
 from jax.sharding import PartitionSpec as P
 
 D = 4096
+
+
+def put_lane_in(u_in, which_dim):
+    u_in = jnp.moveaxis(u_in, 0, which_dim)
+    aux = u_in.shape
+    k_now = u_in.reshape(
+        *aux[:which_dim], aux[which_dim] * aux[which_dim + 1], *aux[which_dim + 2 :]
+    )
+    return k_now
+
+
+def supply_all_spans_in(raw, link_axis):
+    parts_n = lax.axis_size(link_axis)
+    b_now = raw[None]
+    for pp in range(parts_n.bit_length() - 1):
+        u1 = 1 << pp
+        n_now = lax.ppermute(b_now, link_axis, list(map(lambda p: (p, p ^ u1), range(parts_n))))
+        x_new = jnp.stack([b_now, n_now])
+        a_now = lax.axis_index(link_axis) >> pp & 1
+        b_now = jnp.where(a_now == 0, x_new, x_new[::-1]).reshape(-1, *raw.shape)
+    return b_now
+
+
+def carry_matrix(in_array, body, at_axis):
+    v_now = put_lane_in(supply_all_spans_in(in_array, body), at_axis)
+    return v_now
+
+
+list_the_edge = functools.partial(carry_matrix, body="seq", at_axis=1)
 
 
 def passed_along(value, axis, by):
@@ -55,7 +85,7 @@
 
 def local(token_ids, embed_table, norm_gain, short_filters, medium_filters, out_weight):
     section_index = lax.axis_index("section")
-    weight_cols = lax.all_gather(out_weight, "seq", axis=1, tiled=True)[0]
+    weight_cols = list_the_edge(out_weight)[0]
     gain = norm_gain[0]
     shorts = short_filters[0]
     medium = medium_filters[0]

time: 521 us -> 482 us (0.925)
  waiting for transfers between devices: 335 us -> 264 us
  other arithmetic: 6.4 us -> 34.3 us
    all_gather x1 -> x0, waiting for transfers between devices: 87.5 us -> none  [local(): weight_cols = lax.all_gather(out_weight, 'seq', axis=1, tiled=True)[0]]
    all_gather x3, waiting for transfers between devices: 239 us -> 161 us  [mixer_layer(): lax.all_gather(a, 'mp', axis=1, tiled=True)]
    ppermute x0 -> x2, waiting for transfers between devices: none -> 70.7 us  [supply_all_spans_in(): lax.ppermute(b_now, link_axis, list(map(lambda p: (p, p ^ u1), range(part...]
    ppermute x8, waiting for transfers between devices: 7.38 us -> 31.6 us  [passed_along(): return lax.ppermute(value, axis, pairs)]
    another operation x0 -> x3, other arithmetic: none -> 14.3 us  [supply_all_spans_in(): x_new = jnp.stack([b_now, n_now])]
    select_n x0 -> x1, other arithmetic: none -> 13.5 us  [supply_all_spans_in(): b_now = jnp.where(a_now == 0, x_new, x_new[::-1]).reshape(-1, *raw.shape)]
  transfers between devices with their start and end apart: 12 -> 13, of which waited for: 10 -> 9; matrix products, arithmetic and copies ran while one was open for 2% -> 13% of each run, Pallas kernels for 0% -> 0%
where the time goes in v1:
time: 482 us; the launch traced here: 475 us
  waiting for transfers between devices  264 us (55%)
  matrix products  79 us (16%)
  other arithmetic  34.3 us (7%)
  blocking collectives  33.4 us (7%)
  starting transfers between devices  30.3 us (6%)
  local copies, waits for them, and re-layouts  20 us (4%)
  between operations  13.9 us (3%)
    all_gather x3, waiting for transfers between devices, mixer_layer(): lax.all_gather(a, 'mp', axis=1, tiled=True)  161 us
    ppermute x2, waiting for transfers between devices, supply_all_spans_in(): lax.ppermute(b_now, link_axis, list(map(lambda p: (p, p ^ u1), range(part...  70.7 us
    conv_general_dilated x12, matrix products, depthwise(): lax.conv_general_dilated(extended[None], kernel, (1,), 'VALID', dimension...  51.1 us
    psum x3, blocking collectives, mixer_layer(): all_squares = lax.psum(own_squares, 'mp')  33.4 us
    ppermute x8, waiting for transfers between devices, passed_along(): return lax.ppermute(value, axis, pairs)  31.6 us
    dot_general x3, matrix products, mixer_layer(): jnp.dot(piece, block_rows, preferred_element_type=jnp.float32)  26 us
    ppermute x8, starting transfers between devices, passed_along(): return lax.ppermute(value, axis, pairs)  26 us
    another operation x3, other arithmetic, supply_all_spans_in(): x_new = jnp.stack([b_now, n_now])  14.3 us
  transfers between devices with their start and end apart: 13, of which 9 were waited for; matrix products, arithmetic and copies ran while one was open for 13% of the time, Pallas kernels for 0%

profile of v1, /device:TPU:0, one launch (start us, length us, event | category | flops | bytes accessed | tf_op | source)
XLA Modules:
  0.0 474.6 jit_solution(5921552609799342904)
XLA Ops:
  6.5 3.0 collective-permute-start.2
  11.5 12.1 %psum.21 = f32[256,1]{0,1:T(1,128)S(1)} all-reduce(f32[256,1]{0,1:T(1,128)S(1)} %bitcast.130), channel_id=1, replica_groups=mesh['section'=2,'seq'=4,'mp'=4] {'mp'}, use_global_device_ids=true, to_apply=%region_1.2 | all-reduce | flops 256 | bytes 2048 | tf_op jit(solution)/shard_map/psum | solution.py:63
  23.9 2.4 collective-permute-start
  27.1 2.6 rev.31
  29.7 25.3 %collective-permute-done = bf16[6,1024]{1,0:T(8,128)(2,1)S(1)} collective-permute-done((bf16[6,1024]{1,0:T(8,128)(2,1)S(1)}, bf16[6,1024]{1,0:T(8,128)(2,1)S(1)}, u32[]{:S(2)}, u32[]{:S(2)}) %collective-permute-start) | collective-permute-done | bytes 12320 | tf_op jit(solution)/shard_map/ppermute | solution.py:42
  58.4 5.1 %collective-permute-start.1 = (bf16[127,1024]{1,0:T(8,128)(2,1)}, bf16[127,1024]{1,0:T(8,128)(2,1)}, u32[]{:S(2)}, u32[]{:S(2)}) collective-permute-start(bf16[127,1024]{1,0:T(8,128)(2,1)} %slice_bitcast_fusion.5), channel_id=1, source_target_pairs={{0,4},{4,8},{8,12},{1,5},{5,9},{9,13},{2,6},{6,10},{10,14},{3,7},{... | collective-permute-start | bytes 780296 | tf_op jit(solution)/shard_map/ppermute | solution.py:42
  65.1 2.0 pad_maximum_fusion.1
  67.0 4.9 %fusion.1 = (bf16[1,2,1,1024,1024]{4,3,1,2,0:T(8,128)(2,1)}, bf16[2,1,1024,1024]{3,2,0,1:T(8,128)(2,1)}) fusion(bf16[2,1,1,1024,1024]{4,3,2,1,0:T(8,128)(2,1)S(1)} %pad_maximum_fusion.1, pred[]{:T(512)S(6)} %eq.42), kind=kLoop, calls=%fused_computation.5 | loop fusion | flops 2097152 | bytes 12582913 | tf_op jit(solution)/shard_map/stack;reshape | solution.py:25
  73.5 2.3 reshape.130
  77.2 15.2 %fusion.69 = bf16[1,256,1024]{2,0,1:T(2,128)(2,1)} fusion(bf16[1,383,1024]{2,1,0:T(8,128)(2,1)S(1)} %maximum_bitcast_fusion.1, f32[1,264,1024]{2,0,1:T(1,128)S(1)} %copy-done.4, bf16[128,1,1024]{2,0,1:T(8,128)(2,1)S(1)} %bitcast.110), kind=kOutput, calls=%fused_computation.76 | convolution fusion | flops 67633152 | bytes 2619392 | tf_op jit(solution)/shard_map/conv_general_dilated | solution.py:47
  92.9 70.7 %collective-permute-done.3 = bf16[2,1,1024,1024]{3,2,0,1:T(8,128)(2,1)} collective-permute-done((bf16[2,1,1024,1024]{3,2,0,1:T(8,128)(2,1)}, bf16[2,1,1024,1024]{3,2,0,1:T(8,128)(2,1)}, u32[]{:S(2)}, u32[]{:S(2)}) %collective-permute-start.3) | collective-permute-done | bytes 4194336 | tf_op jit(solution)/shard_map/ppermute | solution.py:24
  163.6 7.4 %pad_maximum_fusion = bf16[2,2,1,1024,1024]{4,3,1,2,0:T(8,128)(2,1)} fusion(bf16[1,2,1,1024,1024]{4,3,1,2,0:T(8,128)(2,1)} %bitcast.22, bf16[1,2,1,1024,1024]{4,3,1,2,0:T(8,128)(2,1)} %get-tuple-element.9), kind=kLoop, calls=%fused_computation.1 | loop fusion | flops 4194304 | bytes 16777216 | tf_op jit(solution)/shard_map/stack | solution.py:25
  171.0 13.5 %reverse_select_fusion = bf16[2,2,1,1024,1024]{4,3,1,2,0:T(8,128)(2,1)} fusion(bf16[2,2,1,1024,1024]{4,3,1,2,0:T(8,128)(2,1)} %pad_maximum_fusion, pred[]{:T(512)S(6)} %eq.41), kind=kLoop, calls=%fused_computation | loop fusion | flops 4194304 | bytes 16777216 | tf_op jit(solution)/shard_map/jit(_where)/select_n | solution.py:27
  184.5 8.6 %fusion.47 = bf16[256,1024]{1,0:T(8,128)(2,1)S(1)} fusion(bf16[4096,1024]{1,0:T(8,128)(2,1)} %bitcast.104, bf16[1,256,4096]{2,0,1:T(2,128)(2,1)} %all-gather.7.cloned.1.call-done, bf16[256,1024]{1,0:T(8,128)(2,1)S(1)} %get-tuple-element.17), kind=kOutput, calls=%fused_computation.65 | convolution fusion | flops 2148270080 | bytes 11534336 | tf_op jit(solution)/shard_map/dot_general | solution.py:82
  193.1 1.3 collective-permute-start.4
  194.5 1.5 collective-permute-done.4
  196.0 1.3 fusion.87
  197.3 11.9 %psum.22 = f32[256,1]{0,1:T(1,128)S(1)} all-reduce(f32[256,1]{0,1:T(1,128)S(1)} %bitcast.129), channel_id=1, replica_groups=mesh['section'=2,'seq'=4,'mp'=4] {'mp'}, use_global_device_ids=true, to_apply=%region_3.4 | all-reduce | flops 256 | bytes 2048 | tf_op jit(solution)/shard_map/psum | solution.py:63
  209.4 2.4 collective-permute-start.5
  216.4 4.9 %collective-permute-start.6 = (bf16[127,1024]{1,0:T(8,128)(2,1)}, bf16[127,1024]{1,0:T(8,128)(2,1)}, u32[]{:S(2)}, u32[]{:S(2)}) collective-permute-start(bf16[127,1024]{1,0:T(8,128)(2,1)} %slice_bitcast_fusion.4), channel_id=1, source_target_pairs={{0,4},{4,8},{8,12},{1,5},{5,9},{9,13},{2,6},{6,10},{10,14},{3,7},{... | collective-permute-start | bytes 780296 | tf_op jit(solution)/shard_map/ppermute | solution.py:42
  225.9 15.2 %fusion.75 = bf16[1,256,1024]{2,0,1:T(2,128)(2,1)} fusion(bf16[1,383,1024]{2,1,0:T(8,128)(2,1)S(1)} %maximum_bitcast_fusion.2, f32[1,264,1024]{2,0,1:T(1,128)S(1)} %reshape.131, bf16[128,1,1024]{2,0,1:T(8,128)(2,1)S(1)} %bitcast.111), kind=kOutput, calls=%fused_computation.78 | convolution fusion | flops 67633152 | bytes 2619392 | tf_op jit(solution)/shard_map/conv_general_dilated | solution.py:47
  241.1 81.2 %all-gather.9.cloned.1.call-done = bf16[1,256,4096]{2,0,1:T(2,128)(2,1)} async-done(((bf16[1,256,1024]{2,0,1:T(2,128)(2,1)}), bf16[1,256,4096]{2,0,1:T(2,128)(2,1)}) %all-gather.9.cloned.1.call-update) | async-done | bytes 2097168 | tf_op jit(solution)/shard_map/all_gather | solution.py:80
  322.3 8.6 %fusion.50 = bf16[256,1024]{1,0:T(8,128)(2,1)S(1)} fusion(bf16[4096,1024]{1,0:T(8,128)(2,1)} %bitcast.105, bf16[1,256,4096]{2,0,1:T(2,128)(2,1)} %all-gather.9.cloned.1.call-done, bf16[256,1024]{1,0:T(8,128)(2,1)S(1)} %copy-done.7), kind=kOutput, calls=%fused_computation.66 | convolution fusion | flops 2148270080 | bytes 11534336 | tf_op jit(solution)/shard_map/dot_general | solution.py:82
  330.9 1.3 collective-permute-start.7
  332.3 1.5 collective-permute-done.7
  334.0 9.4 %psum.23 = f32[256,1]{0,1:T(1,128)S(1)} all-reduce(f32[256,1]{0,1:T(1,128)S(1)} %bitcast.125), channel_id=1, replica_groups=mesh['section'=2,'seq'=4,'mp'=4] {'mp'}, use_global_device_ids=true, to_apply=%region_5.6 | all-reduce | flops 256 | bytes 2048 | tf_op jit(solution)/shard_map/psum | solution.py:63
  343.6 3.6 collective-permute-start.8
  351.7 4.9 %collective-permute-start.9 = (bf16[127,1024]{1,0:T(8,128)(2,1)}, bf16[127,1024]{1,0:T(8,128)(2,1)}, u32[]{:S(2)}, u32[]{:S(2)}) collective-permute-start(bf16[127,1024]{1,0:T(8,128)(2,1)} %slice_bitcast_fusion.3), channel_id=1, source_target_pairs={{0,4},{4,8},{8,12},{1,5},{5,9},{9,13},{2,6},{6,10},{10,14},{3,7},{... | collective-permute-start | bytes 780296 | tf_op jit(solution)/shard_map/ppermute | solution.py:42
  357.8 2.4 reshape.132
  361.6 15.2 %fusion.81 = bf16[1,256,1024]{2,0,1:T(2,128)(2,1)} fusion(bf16[1,383,1024]{2,1,0:T(8,128)(2,1)S(1)} %maximum_bitcast_fusion.3, f32[1,264,1024]{2,0,1:T(1,128)S(1)} %copy-done.3, bf16[128,1,1024]{2,0,1:T(8,128)(2,1)S(1)} %bitcast.112), kind=kOutput, calls=%fused_computation.80 | convolution fusion | flops 67633152 | bytes 2619392 | tf_op jit(solution)/shard_map/conv_general_dilated | solution.py:47
  377.8 80.3 %all-gather.11.cloned.1.call-done = bf16[1,256,4096]{2,0,1:T(2,128)(2,1)} async-done(((bf16[1,256,1024]{2,0,1:T(2,128)(2,1)}), bf16[1,256,4096]{2,0,1:T(2,128)(2,1)}) %all-gather.11.cloned.1.call-update) | async-done | bytes 2097168 | tf_op jit(solution)/shard_map/all_gather | solution.py:80
  458.1 8.7 %fusion.63 = bf16[1,256,1024]{2,1,0:T(8,128)(2,1)S(1)} fusion(bf16[256,1024]{1,0:T(8,128)(2,1)S(1)} %fusion.50, bf16[4096,1024]{1,0:T(8,128)(2,1)} %bitcast.106, bf16[1,256,4096]{2,0,1:T(2,128)(2,1)} %all-gather.11.cloned.1.call-done, bf16[256,1024]{1,0:T(8,128)(2,1)S(1)} %get-tuple-element.6, pred[]{:T(512)S(6)} %eq.18), kind=kOutput, calls=%fused_computation.74 | convolution fusion | flops 2148532224 | bytes 12058625 | tf_op jit(solution)/shard_map/dot_general | solution.py:82
  (108 shorter events, 30.2 us)
Async XLA Ops:
  6.5 4.4 copy-start
  6.5 178.0 %all-gather.7.cloned.1.call-start = ((), (), s32[]{:S(2)}) async-start(), calls=%async_computation | async-start | bytes 5242880 | tf_op jit(solution)/shard_map/all_gather | solution.py:80
  6.5 57.5 %collective-permute-start.2 = (bf16[1,1,1024,1024]{3,2,1,0:T(8,128)(2,1)}, bf16[1,1,1024,1024]{3,2,1,0:T(8,128)(2,1)}, u32[]{:S(2)}, u32[]{:S(2)}) collective-permute-start(bf16[1,1,1024,1024]{3,2,1,0:T(8,128)(2,1)} %bitcast.107), channel_id=1, source_target_pairs={{0,4},{4,0},{8,12},{12,8},{1,5},{5,1},{9,13},{13,9},{2,6},{6,2},{1... | collective-permute-start | bytes 6291464 | tf_op jit(solution)/shard_map/ppermute | solution.py:24
  11.0 15.4 %copy-start.14 = (bf16[1,3,7,1024]{3,2,1,0:T(8,128)(2,1)S(1)}, bf16[1,3,7,1024]{3,2,1,0:T(8,128)(2,1)}, u32[]{:S(2)}) copy-start(bf16[1,3,7,1024]{3,2,1,0:T(8,128)(2,1)} %param.9) | copy-start | bytes 129028
  11.5 15.6 %copy-start.10 = (bf16[1,128,1024]{2,1,0:T(8,128)(2,1)S(1)}, bf16[1,128,1024]{2,1,0:T(8,128)(2,1)}, u32[]{:S(2)}) copy-start(bf16[1,128,1024]{2,1,0:T(8,128)(2,1)} %param.10) | copy-start | bytes 786436
  23.9 31.1 %collective-permute-start = (bf16[6,1024]{1,0:T(8,128)(2,1)S(1)}, bf16[6,1024]{1,0:T(8,128)(2,1)S(1)}, u32[]{:S(2)}, u32[]{:S(2)}) collective-permute-start(bf16[6,1024]{1,0:T(8,128)(2,1)S(1)} %slice.84), channel_id=1, source_target_pairs={{0,4},{4,8},{8,12},{1,5},{5,9},{9,13},{2,6},{6,10},{10,14},{3,7},{... | collective-permute-start | bytes 36872 | tf_op jit(solution)/shard_map/ppermute | solution.py:42
  55.1 0.7 copy-start.15
  58.4 17.4 %collective-permute-start.1 = (bf16[127,1024]{1,0:T(8,128)(2,1)}, bf16[127,1024]{1,0:T(8,128)(2,1)}, u32[]{:S(2)}, u32[]{:S(2)}) collective-permute-start(bf16[127,1024]{1,0:T(8,128)(2,1)} %slice_bitcast_fusion.5), channel_id=1, source_target_pairs={{0,4},{4,8},{8,12},{1,5},{5,9},{9,13},{2,6},{6,10},{10,14},{3,7},{... | collective-permute-start | bytes 780296 | tf_op jit(solution)/shard_map/ppermute | solution.py:42
  63.5 1.6 copy-start.2
  72.0 91.6 %collective-permute-start.3 = (bf16[2,1,1024,1024]{3,2,0,1:T(8,128)(2,1)}, bf16[2,1,1024,1024]{3,2,0,1:T(8,128)(2,1)}, u32[]{:S(2)}, u32[]{:S(2)}) collective-permute-start(bf16[2,1,1024,1024]{3,2,0,1:T(8,128)(2,1)} %get-tuple-element.10), channel_id=1, source_target_pairs={{0,8},{4,12},{8,0},{12,4},{1,9},{5,13},{9,1},{13,5},{2,10},{6,14},... | collective-permute-start | bytes 12582920 | tf_op jit(solution)/shard_map/ppermute | solution.py:24
  75.8 1.3 copy-start.4
  75.8 1.4 copy-start.11
  92.3 229.9 %all-gather.9.cloned.1.call-start = ((), (), s32[]{:S(2)}) async-start(), calls=%async_computation.1 | async-start | bytes 5242880 | tf_op jit(solution)/shard_map/all_gather | solution.py:80
  193.1 4.1 copy-start.8
  193.1 2.8 collective-permute-start.4
  197.3 15.8 %copy-start.6 = (bf16[256,1024]{1,0:T(8,128)(2,1)}, bf16[256,1024]{1,0:T(8,128)(2,1)S(1)}, u32[]{:S(2)}) copy-start(bf16[256,1024]{1,0:T(8,128)(2,1)S(1)} %get-tuple-element.8) | copy-start | bytes 1572868
  209.4 3.7 collective-permute-start.5
  216.4 8.4 %collective-permute-start.6 = (bf16[127,1024]{1,0:T(8,128)(2,1)}, bf16[127,1024]{1,0:T(8,128)(2,1)}, u32[]{:S(2)}, u32[]{:S(2)}) collective-permute-start(bf16[127,1024]{1,0:T(8,128)(2,1)} %slice_bitcast_fusion.4), channel_id=1, source_target_pairs={{0,4},{4,8},{8,12},{1,5},{5,9},{9,13},{2,6},{6,10},{10,14},{3,7},{... | collective-permute-start | bytes 780296 | tf_op jit(solution)/shard_map/ppermute | solution.py:42
  223.8 2.0 copy-start.12
  225.9 96.4 %copy-start.7 = (bf16[256,1024]{1,0:T(8,128)(2,1)S(1)}, bf16[256,1024]{1,0:T(8,128)(2,1)}, u32[]{:S(2)}) copy-start(bf16[256,1024]{1,0:T(8,128)(2,1)} %copy-done.6) | copy-start | bytes 1572868
  241.1 92.7 %copy-start.5 = (bf16[256,1024]{1,0:T(8,128)(2,1)S(1)}, bf16[256,1024]{1,0:T(8,128)(2,1)}, u32[]{:S(2)}) copy-start(bf16[256,1024]{1,0:T(8,128)(2,1)} %get-tuple-element.18) | copy-start | bytes 1572868
  241.1 217.0 %all-gather.11.cloned.1.call-start = ((), (), s32[]{:S(2)}) async-start(), calls=%async_computation.2 | async-start | bytes 5242880 | tf_op jit(solution)/shard_map/all_gather | solution.py:80
  330.9 2.8 collective-permute-start.7
  343.6 4.8 %collective-permute-start.8 = (bf16[6,1024]{1,0:T(8,128)(2,1)S(1)}, bf16[6,1024]{1,0:T(8,128)(2,1)S(1)}, u32[]{:S(2)}, u32[]{:S(2)}) collective-permute-start(bf16[6,1024]{1,0:T(8,128)(2,1)S(1)} %slice.94), channel_id=1, source_target_pairs={{0,4},{4,8},{8,12},{1,5},{5,9},{9,13},{2,6},{6,10},{10,14},{3,7},{... | collective-permute-start | bytes 36872 | tf_op jit(solution)/shard_map/ppermute | solution.py:42
  351.7 8.6 %collective-permute-start.9 = (bf16[127,1024]{1,0:T(8,128)(2,1)}, bf16[127,1024]{1,0:T(8,128)(2,1)}, u32[]{:S(2)}, u32[]{:S(2)}) collective-permute-start(bf16[127,1024]{1,0:T(8,128)(2,1)} %slice_bitcast_fusion.3), channel_id=1, source_target_pairs={{0,4},{4,8},{8,12},{1,5},{5,9},{9,13},{2,6},{6,10},{10,14},{3,7},{... | collective-permute-start | bytes 780296 | tf_op jit(solution)/shard_map/ppermute | solution.py:42
  360.2 1.3 copy-start.3
  360.2 1.4 copy-start.13
  376.7 1.0 copy-start.9
  458.1 9.8 %copy-start.1 = (bf16[512,1024]{1,0:T(8,128)(2,1)S(1)}, bf16[512,1024]{1,0:T(8,128)(2,1)}, u32[]{:S(2)}) copy-start(bf16[512,1024]{1,0:T(8,128)(2,1)} %param.7) | copy-start | bytes 3145732
Sparse Core Ops, SparseCore 0:
  92.5 80.7 all-gather.6
  241.2 81.0 all-gather.8
  376.9 81.1 all-gather.10
